TPU v7x, 8 devices: a whole 2x2x1 slice. The times are simulated.
8 devices in a mesh: dp: 2 (over z, y), sp: 4 (over x, core).
Axes of the slice: x: 2, y: 2, z: 1, core: 2. Of those that a mesh axis runs over, the one named last changes fastest.
Arguments:
- latents: bfloat16 [6, 96, 256, 768], P('dp', 'sp'), parts along dimension 0
- text_ctx: bfloat16 [6, 120, 768], P('dp'), parts along dimension 0
- modulation: float32 [6, 6, 768], P('dp'), parts along dimension 0
- pos_temporal: float32 [96, 768], replicated
- w_qkv_spatial: bfloat16 [3, 12, 64, 768], replicated
- w_out_spatial: bfloat16 [12, 64, 768], replicated
- w_qkv_temporal: bfloat16 [3, 12, 64, 768], replicated
- w_out_temporal: bfloat16 [12, 64, 768], replicated
- w_query_cross: bfloat16 [12, 64, 768], replicated
- w_kv_cross: bfloat16 [2, 12, 64, 768], replicated
- w_out_cross: bfloat16 [12, 64, 768], replicated
- w_mlp_in: bfloat16 [768, 3072], replicated
- w_mlp_out: bfloat16 [3072, 768], replicated
Outputs:
- output: bfloat16 [6, 96, 256, 768], P('dp', 'sp'), parts along dimension 0
There are 2 independent parts. A program takes and returns all parts, laid end to end along the dimension named above; an argument that names none is the same for every part.
All inputs are finite; a program needn't handle non-finite values.
Results may differ from a plain program's by a relative error of at most 0.0143476.
Values are sent between devices in bfloat16 or wider.
A program may use at most 1 GiB of HBM per device.

v0:
```python
import jax
import jax.numpy as jnp
from jax import lax
from jax.sharding import PartitionSpec as P

LN_EPS = 1e-6


def layer_norm(acts_in):
    centered = acts_in - jnp.mean(acts_in, axis=-1, keepdims=True)
    return centered * lax.rsqrt(jnp.mean(centered * centered, axis=-1, keepdims=True) + LN_EPS)


def spatial_sublayer(latents, mod_rows, w_qkv, w_out):
    head_dim = w_out.shape[1]
    lat_f = latents.astype(jnp.float32)
    normed = (layer_norm(lat_f) * (1.0 + mod_rows[1]) + mod_rows[0]).astype(jnp.bfloat16)
    qkv_all = jnp.einsum('btsc,jhdc->jbtshd', normed, w_qkv, preferred_element_type=jnp.float32).astype(jnp.bfloat16)
    scores = jnp.einsum('btqhd,btkhd->bthqk', qkv_all[0], qkv_all[1], preferred_element_type=jnp.float32)
    attn_probs = jax.nn.softmax(scores * (head_dim ** -0.5), axis=-1).astype(jnp.bfloat16)
    mixed_out = jnp.einsum('bthqk,btkhd->btqhd', attn_probs, qkv_all[2], preferred_element_type=jnp.float32).astype(jnp.bfloat16)
    branch = jnp.einsum('btshd,hdc->btsc', mixed_out, w_out, preferred_element_type=jnp.float32)
    return (lat_f + mod_rows[2] * branch).astype(jnp.bfloat16)


def temporal_sublayer(hidden, pos_temporal, gate_row, w_qkv, w_out):
    head_dim = w_out.shape[1]
    hid_f = hidden.astype(jnp.float32)
    shifted = (hid_f + pos_temporal[None, :, None, :]).astype(jnp.bfloat16)
    qkv_all = jnp.einsum('btsc,jhdc->jbtshd', shifted, w_qkv, preferred_element_type=jnp.float32).astype(jnp.bfloat16)
    scores = jnp.einsum('bqshd,bkshd->bshqk', qkv_all[0], qkv_all[1], preferred_element_type=jnp.float32)
    attn_probs = jax.nn.softmax(scores * (head_dim ** -0.5), axis=-1).astype(jnp.bfloat16)
    mixed_out = jnp.einsum('bshqk,bkshd->bqshd', attn_probs, qkv_all[2], preferred_element_type=jnp.float32).astype(jnp.bfloat16)
    branch = jnp.einsum('btshd,hdc->btsc', mixed_out, w_out, preferred_element_type=jnp.float32)
    return (hid_f + gate_row * branch).astype(jnp.bfloat16)


def cross_mlp(hidden, ctx_kv, mod_rows, w_query_cross, w_out_cross, w_mlp_in, w_mlp_out):
    head_dim = w_out_cross.shape[1]
    hid_f = hidden.astype(jnp.float32)
    query_heads = jnp.einsum('btsc,hdc->btshd', hidden, w_query_cross, preferred_element_type=jnp.float32).astype(jnp.bfloat16)
    scores = jnp.einsum('btshd,blhd->bthsl', query_heads, ctx_kv[0], preferred_element_type=jnp.float32)
    attn_probs = jax.nn.softmax(scores * (head_dim ** -0.5), axis=-1).astype(jnp.bfloat16)
    mixed_out = jnp.einsum('bthsl,blhd->btshd', attn_probs, ctx_kv[1], preferred_element_type=jnp.float32).astype(jnp.bfloat16)
    after_cross = (hid_f + jnp.einsum('btshd,hdc->btsc', mixed_out, w_out_cross, preferred_element_type=jnp.float32)).astype(jnp.bfloat16)
    cross_f = after_cross.astype(jnp.float32)
    normed = (layer_norm(cross_f) * (1.0 + mod_rows[4]) + mod_rows[3]).astype(jnp.bfloat16)
    mlp_hidden = jax.nn.gelu(jnp.einsum('btsc,cf->btsf', normed, w_mlp_in, preferred_element_type=jnp.float32), approximate=True).astype(jnp.bfloat16)
    mlp_out = jnp.einsum('btsf,fc->btsc', mlp_hidden, w_mlp_out, preferred_element_type=jnp.float32)
    return (cross_f + mod_rows[5] * mlp_out).astype(jnp.bfloat16)


def solution(mesh):
    act_spec = P('dp', 'sp', None, None)
    row_spec = P('dp', None, None)
    rep_two = P(None, None)
    rep_three = P(None, None, None)
    rep_four = P(None, None, None, None)
    in_specs = (act_spec, row_spec, row_spec, rep_two, rep_four, rep_three, rep_four, rep_three, rep_three, rep_four, rep_three, rep_two, rep_two)

    def local_block(latents, text_ctx, modulation, pos_temporal, w_qkv_spatial, w_out_spatial, w_qkv_temporal, w_out_temporal, w_query_cross, w_kv_cross, w_out_cross, w_mlp_in, w_mlp_out):
        mod_rows = jnp.moveaxis(modulation, 1, 0)[:, :, None, None, :]
        after_spatial = spatial_sublayer(latents, mod_rows, w_qkv_spatial, w_out_spatial)
        by_patch = lax.all_to_all(after_spatial, 'sp', 2, 1, tiled=True)
        after_temporal = temporal_sublayer(by_patch, pos_temporal, mod_rows[2], w_qkv_temporal, w_out_temporal)
        by_frame = lax.all_to_all(after_temporal, 'sp', 1, 2, tiled=True)
        ctx_kv = jnp.einsum('blc,jhdc->jblhd', text_ctx, w_kv_cross, preferred_element_type=jnp.float32).astype(jnp.bfloat16)
        return cross_mlp(by_frame, ctx_kv, mod_rows, w_query_cross, w_out_cross, w_mlp_in, w_mlp_out)

    return jax.shard_map(local_block, mesh=mesh, in_specs=in_specs, out_specs=act_spec, check_vma=False)
```

profile of v0, /device:TPU:0, one launch (start us, length us, event | category | flops | bytes accessed | tf_op | source)
XLA Modules:
  0.0 2274.9 jit_solution(7057692595790419786)
XLA Ops:
  0.0 0.0 copy-start
  0.0 1.9 fusion.132
  1.9 10.4 convert_reduce_fusion.1
  12.3 0.0 copy-start.4
  12.3 0.6 copy-done.4
  12.9 12.4 fusion.36
  25.4 0.7 add_rsqrt_fusion.1
  26.0 0.6 copy_bitcast_fusion.3
  26.6 0.0 copy-done
  26.6 76.2 %convert_bitcast_fusion.1 = bf16[3,3,24,256,12,64]{3,5,4,0,2,1:T(8,128)(2,1)} fusion(bf16[3,24,256,768]{3,2,1,0:T(8,128)(2,1)} %param.13, f32[3,768]{1,0:T(4,128)S(1)} %get-tuple-element.24, f32[3,768]{1,0:T(4,128)} %get-tuple-element.25, f32[3,24,256]{2,1,0:T(8,128)} %add_rsqrt_fusion.1, f32[3,24,256]{2,1,0:T(8,128)} %copy-done.4, ...), kind=kOutput, calls=%fused_computation.34 | convolution fusion | flops 65357217792 | bytes 116951040 | tf_op jit(solution)/shard_map/btsc,jhdc->jbtshd/dot_general | solution.py:18
  102.8 0.0 copy-start.8
  102.8 0.0 copy-start.15
  102.8 100.2 %fusion.133 = (f32[3,24,12,256]{3,2,1,0:T(8,128)S(1)}, f32[3,24,12,256,256]{3,4,2,1,0:T(8,128)}) fusion(bf16[3,3,24,256,12,64]{3,5,4,0,2,1:T(8,128)(2,1)} %convert_bitcast_fusion.1), kind=kOutput, calls=%fused_computation.136 | convolution fusion | flops 7417626624 | bytes 284000256 | tf_op jit(solution)/shard_map/sub | solution.py:20
  203.0 0.0 copy-done.8
  203.0 0.0 copy-start.12
  203.0 0.0 copy-done.15
  203.0 96.3 %fusion.40 = bf16[3,24,256,768]{3,2,1,0:T(8,128)(2,1)} fusion(bf16[3,24,256,768]{3,2,1,0:T(8,128)(2,1)} %param.13, f32[3,24,12,256,256]{3,4,2,1,0:T(8,128)} %get-tuple-element.17, f32[3,24,12,256]{3,2,1,0:T(8,128)S(1)} %get-tuple-element.16, bf16[3,3,24,256,12,64]{3,5,4,0,2,1:T(8,128)(2,1)} %convert_bitcast_fusion.1, f32[3,768]{1,0:T(4,128)S(1)} %bitcast.221, ...), kind=kOutput, calls=%fused_computation.50 | convolution fusion | flops 29175054336 | bytes 313500672 | tf_op jit(solution)/shard_map/btshd,hdc->btsc/dot_general | solution.py:22
  299.4 0.0 copy-done.12
  299.4 19.4 copy.19
  318.8 313.4 %all_to_all.27 = bf16[3,24,256,768]{3,1,0,2:T(8,128)(2,1)S(1)} all-to-all(bf16[3,24,256,768]{3,1,0,2:T(8,128)(2,1)} %copy.19), channel_id=1, replica_groups=mesh['dp'=2,'sp'=4] {'sp'}, dimensions={2} | all-to-all | bytes 56623104 | tf_op jit(solution)/shard_map/all_to_all | solution.py:64
  632.1 0.0 copy-start.14
  632.1 18.3 copy.20
  650.5 0.0 copy-done.14
  650.5 141.7 %convert_bitcast_fusion = bf16[3,3,96,64,12,64]{5,3,4,0,2,1:T(8,128)(2,1)} fusion(f32[3,96,64,768]{3,2,1,0:T(8,128)} %bitcast.217, f32[96,768]{1,0:T(8,128)} %param.16, bf16[3,12,64,768]{3,2,1,0:T(8,128)(2,1)S(1)} %copy-done.14), kind=kOutput, calls=%fused_computation.16 | convolution fusion | flops 65300594688 | bytes 145391616 | tf_op jit(solution)/shard_map/btsc,jhdc->jbtshd/dot_general | solution.py:30
  792.1 139.7 %slice_bitcast_fusion.1 = (bf16[3,96,64,12,64]{4,2,3,1,0:T(8,128)(2,1)}, bf16[3,96,64,12,64]{4,2,3,1,0:T(8,128)(2,1)}, bf16[3,96,64,12,64]{4,2,3,1,0:T(8,128)(2,1)}) fusion(bf16[3,3,96,64,12,64]{5,3,4,0,2,1:T(8,128)(2,1)} %convert_bitcast_fusion), kind=kLoop, calls=%fused_computation.53 | loop fusion | bytes 169869312 | tf_op jit(solution)/shard_map/squeeze | solution.py:31
  931.8 170.1 %fusion.49 = f32[3,64,12,96,96]{3,4,2,1,0:T(8,128)} fusion(bf16[3,96,64,12,64]{4,2,3,1,0:T(8,128)(2,1)} %get-tuple-element.6, bf16[3,96,64,12,64]{4,2,3,1,0:T(8,128)(2,1)} %get-tuple-element.5), kind=kOutput, calls=%fused_computation.65 | convolution fusion | flops 2717908992 | bytes 141557760 | tf_op jit(solution)/shard_map/bqshd,bkshd->bshqk/dot_general | solution.py:31
  1101.9 112.4 %fusion.134 = (f32[3,64,12,96]{3,2,1,0:T(8,128)S(1)}, f32[3,64,12,96,96]{3,4,2,1,0:T(8,128)}) fusion(f32[3,64,12,96,96]{3,4,2,1,0:T(8,128)} %fusion.49), kind=kOutput, calls=%fused_computation.137 | output fusion | flops 84934752 | bytes 170754048 | tf_op jit(solution)/shard_map/sub | solution.py:32
  1214.3 97.4 %fusion.47 = bf16[3,64,12,64,96]{4,3,2,1,0:T(8,128)(2,1)} fusion(bf16[3,96,64,12,64]{4,2,3,1,0:T(8,128)(2,1)} %get-tuple-element.7, f32[3,64,12,96,96]{3,4,2,1,0:T(8,128)} %get-tuple-element.19, f32[3,64,12,96]{3,2,1,0:T(8,128)S(1)} %get-tuple-element.18), kind=kOutput, calls=%fused_computation.63 | convolution fusion | flops 2760376320 | bytes 142442496 | tf_op jit(solution)/shard_map/bshqk,bkshd->bqshd/dot_general | solution.py:33
  1311.7 0.0 copy-start.16
  1311.7 88.6 %copy.33 = bf16[3,64,12,64,96]{3,1,2,4,0:T(8,128)(2,1)} copy(bf16[3,64,12,64,96]{4,3,2,1,0:T(8,128)(2,1)} %fusion.47) | data formatting | bytes 56623104 | tf_op jit(solution)/shard_map/bshqk,bkshd->bqshd/dot_general | solution.py:33
  1400.3 0.0 copy-done.13
  1400.3 0.0 copy-done.16
  1400.3 48.3 %fusion.44 = bf16[3,96,64,768]{3,2,1,0:T(8,128)(2,1)} fusion(f32[3,96,64,768]{3,2,1,0:T(8,128)} %bitcast.218, bf16[3,64,12,64,96]{3,1,2,4,0:T(8,128)(2,1)} %copy.33, f32[3,768]{1,0:T(4,128)S(1)} %bitcast.222, bf16[12,64,768]{2,1,0:T(8,128)(2,1)S(1)} %copy-done.16), kind=kOutput, calls=%fused_computation.59 | convolution fusion | flops 21785739264 | bytes 114435072 | tf_op jit(solution)/shard_map/btshd,hdc->btsc/dot_general | solution.py:34
  1448.6 0.0 copy-start.7
  1448.6 0.0 copy-start.5
  1448.6 0.0 copy-start.6
  1448.6 0.0 copy-start.18
  1448.6 19.6 copy.23
  1468.2 9.1 all-to-all-start.1
  1477.3 0.0 copy-done.7
  1477.3 0.6 copy.84
  1477.9 0.0 copy-done.5
  1477.9 0.0 copy-done.6
  1477.9 0.6 copy_bitcast_fusion
  1478.5 0.0 copy-done.18
  1478.5 3.1 fusion.113
  1481.6 0.9 slice_bitcast_fusion.22
  1482.6 301.0 %all-to-all-done.1 = bf16[3,96,64,768]{3,2,0,1:T(8,128)(2,1)} async-done(((bf16[3,96,64,768]{3,2,0,1:T(8,128)(2,1)}), bf16[3,96,64,768]{3,2,0,1:T(8,128)(2,1)}, u32[]{:S(2)}, u32[]{:S(2)}) %all-to-all-start.1) | async-done | bytes 28311584 | tf_op jit(solution)/shard_map/all_to_all | solution.py:66
  1783.6 19.3 copy.24
  1802.9 0.0 copy-done.2
  1802.9 51.0 %fusion.86 = f32[3,12,120,24,256]{4,2,3,1,0:T(8,128)} fusion(bf16[3,24,256,768,1]{3,2,1,4,0:T(8,128)(2,1)} %bitcast.215, bf16[12,64,768]{2,1,0:T(8,128)(2,1)S(1)} %copy-done.2, bf16[3,120,12,64,1]{1,3,0,2,4:T(8,128)(2,1)S(1)} %get-tuple-element.9), kind=kOutput, calls=%fused_computation.89 | convolution fusion | flops 25154813952 | bytes 136212480 | tf_op jit(solution)/shard_map/btshd,blhd->bthsl/dot_general | solution.py:42
  1853.9 102.7 %fusion.135 = (f32[3,24,12,256]{3,1,2,0:T(8,128)S(1)}, f32[3,24,12,256,120]{3,4,1,2,0:T(8,128)}) fusion(f32[3,12,120,24,256]{4,2,3,1,0:T(8,128)} %fusion.86), kind=kOutput, calls=%fused_computation.138 | output fusion | flops 106168440 | bytes 213221376 | tf_op jit(solution)/shard_map/sub | solution.py:43
  1956.6 0.0 copy-done.3
  1956.6 0.0 copy-done.17
  1956.6 56.6 %fusion.42 = bf16[3,24,256,768]{3,2,1,0:T(8,128)(2,1)} fusion(bf16[3,4,24,64,768]{4,3,1,2,0:T(8,128)(2,1)} %copy.24, bf16[12,64,768]{2,1,0:T(8,128)(2,1)S(1)} %copy-done.17, bf16[3,120,12,64,1]{1,3,0,2,4:T(8,128)(2,1)S(1)} %copy-done.3, f32[3,24,12,256,120]{3,4,1,2,0:T(8,128)} %get-tuple-element.21, f32[3,24,12,256]{3,1,2,0:T(8,128)S(1)} %get-tuple-element.20), kind=kOutput, calls=%fused_computation.56 | convolution fusion | flops 25250365440 | bytes 165408768 | tf_op jit(solution)/shard_map/btshd,hdc->btsc/dot_general | solution.py:45
  2013.2 10.4 convert_reduce_fusion
  2023.6 12.5 fusion.32
  2036.1 0.0 copy-done.10
  2036.1 0.0 copy-done.11
  2036.2 0.0 copy-start.9
  2036.2 138.6 %fusion.170 = bf16[3,24,256,3072]{3,2,1,0:T(8,128)(2,1)} fusion(bf16[3,24,256,768]{3,2,1,0:T(8,128)(2,1)} %fusion.42, f32[3,768]{1,0:T(4,128)S(1)} %copy-done.10, f32[3,768]{1,0:T(4,128)S(1)} %copy-done.11, f32[3,24,256]{2,1,0:T(8,128)S(1)} %add_rsqrt_fusion, f32[3,24,256]{2,1,0:T(8,128)S(1)} %broadcast_multiply_fusion, ...), kind=kOutput, calls=%fused_computation.11.clone.clone.clone.clone.1 | convolution fusion | flops 87567630336 | bytes 146442240 | tf_op jit(solution)/shard_map/btsc,cf->btsf/dot_general | solution.py:48
  2174.7 0.0 copy-done.9
  2174.7 99.8 %fusion.41 = bf16[3,24,256,768]{3,2,1,0:T(8,128)(2,1)} fusion(bf16[3,24,256,768]{3,2,1,0:T(8,128)(2,1)} %fusion.42, f32[3,768]{1,0:T(4,128)S(1)} %bitcast.220, bf16[3072,768]{1,0:T(8,128)(2,1)} %param.25, bf16[3,24,256,3072]{3,2,1,0:T(8,128)(2,1)} %fusion.170), kind=kOutput, calls=%fused_computation.51 | convolution fusion | flops 87029710848 | bytes 174597120 | tf_op jit(solution)/shard_map/btsf,fc->btsc/dot_general | solution.py:49
  2274.5 0.0 copy-done.1
  (11 shorter events, 0.1 us)
Async XLA Ops:
  0.0 26.6 %copy-start = (bf16[3,12,64,768]{3,2,1,0:T(8,128)(2,1)S(1)}, bf16[3,12,64,768]{3,2,1,0:T(8,128)(2,1)}, u32[]{:S(2)}) copy-start(bf16[3,12,64,768]{3,2,1,0:T(8,128)(2,1)} %param.17) | copy-start | bytes 10616836
  12.3 0.6 copy-start.4
  102.8 100.2 %copy-start.8 = (f32[1,3,768]{2,0,1:T(1,128)S(1)}, f32[1,3,768]{2,0,1:T(1,128)}, u32[]{:S(2)}) copy-start(f32[1,3,768]{2,0,1:T(1,128)} %get-tuple-element.15) | copy-start | bytes 27652
  102.8 100.3 %copy-start.15 = (bf16[12,64,768]{2,1,0:T(8,128)(2,1)S(1)}, bf16[12,64,768]{2,1,0:T(8,128)(2,1)}, u32[]{:S(2)}) copy-start(bf16[12,64,768]{2,1,0:T(8,128)(2,1)} %param.18) | copy-start | bytes 3538948
  203.0 96.4 %copy-start.12 = (f32[1,3,768]{2,1,0:T(4,128)}, f32[1,3,768]{2,1,0:T(4,128)S(1)}, u32[]{:S(2)}) copy-start(f32[1,3,768]{2,1,0:T(4,128)S(1)} %copy.85) | copy-start | bytes 27652
  632.1 18.3 copy-start.14
  1311.7 88.6 %copy-start.13 = (f32[1,3,768]{2,1,0:T(4,128)S(1)}, f32[1,3,768]{2,1,0:T(4,128)}, u32[]{:S(2)}) copy-start(f32[1,3,768]{2,1,0:T(4,128)} %copy-done.12) | copy-start | bytes 27652
  1311.7 88.6 %copy-start.16 = (bf16[12,64,768]{2,1,0:T(8,128)(2,1)S(1)}, bf16[12,64,768]{2,1,0:T(8,128)(2,1)}, u32[]{:S(2)}) copy-start(bf16[12,64,768]{2,1,0:T(8,128)(2,1)} %param.20) | copy-start | bytes 3538948
  1448.6 28.8 %copy-start.7 = (f32[1,3,768]{2,0,1:T(1,128)S(1)}, f32[1,3,768]{2,0,1:T(1,128)}, u32[]{:S(2)}) copy-start(f32[1,3,768]{2,0,1:T(1,128)} %get-tuple-element.10) | copy-start | bytes 27652
  1448.6 29.4 %copy-start.5 = (f32[1,3,768]{2,0,1:T(1,128)S(1)}, f32[1,3,768]{2,0,1:T(1,128)}, u32[]{:S(2)}) copy-start(f32[1,3,768]{2,0,1:T(1,128)} %get-tuple-element.11) | copy-start | bytes 27652
  1448.6 29.4 %copy-start.6 = (f32[1,3,768]{2,0,1:T(1,128)S(1)}, f32[1,3,768]{2,0,1:T(1,128)}, u32[]{:S(2)}) copy-start(f32[1,3,768]{2,0,1:T(1,128)} %get-tuple-element.12) | copy-start | bytes 27652
  1448.6 30.0 %copy-start.18 = (bf16[3,120,768]{2,1,0:T(8,128)(2,1)S(1)}, bf16[3,120,768]{2,1,0:T(8,128)(2,1)}, u32[]{:S(2)}) copy-start(bf16[3,120,768]{2,1,0:T(8,128)(2,1)} %param.14) | copy-start | bytes 1658884
  1468.2 334.7 %copy-start.2 = (bf16[12,64,768]{2,1,0:T(8,128)(2,1)S(1)}, bf16[12,64,768]{2,1,0:T(8,128)(2,1)}, u32[]{:S(2)}) copy-start(bf16[12,64,768]{2,1,0:T(8,128)(2,1)} %param.21) | copy-start | bytes 3538948
  1468.2 315.4 %all-to-all-start.1 = ((bf16[3,96,64,768]{3,2,0,1:T(8,128)(2,1)}), bf16[3,96,64,768]{3,2,0,1:T(8,128)(2,1)}, u32[]{:S(2)}, u32[]{:S(2)}) async-start(bf16[3,96,64,768]{3,2,0,1:T(8,128)(2,1)} %copy.23), calls=%async_computation.1 | async-start | bytes 56623104 | tf_op jit(solution)/shard_map/all_to_all | solution.py:66
  1853.9 102.7 %copy-start.3 = (bf16[3,120,12,64,1]{1,3,0,2,4:T(8,128)(2,1)S(1)}, bf16[3,120,12,64,1]{1,3,0,2,4:T(8,128)(2,1)}, u32[]{:S(2)}) copy-start(bf16[3,120,12,64,1]{1,3,0,2,4:T(8,128)(2,1)} %get-tuple-element.8) | copy-start | bytes 1658884
  1853.9 102.7 %copy-start.17 = (bf16[12,64,768]{2,1,0:T(8,128)(2,1)S(1)}, bf16[12,64,768]{2,1,0:T(8,128)(2,1)}, u32[]{:S(2)}) copy-start(bf16[12,64,768]{2,1,0:T(8,128)(2,1)} %param.23) | copy-start | bytes 3538948
  2013.2 22.9 %copy-start.10 = (f32[3,768]{1,0:T(4,128)S(1)}, f32[3,768]{1,0:T(4,128)}, u32[]{:S(2)}) copy-start(f32[3,768]{1,0:T(4,128)} %get-tuple-element.22) | copy-start | bytes 27652
  2013.2 22.9 %copy-start.11 = (f32[3,768]{1,0:T(4,128)S(1)}, f32[3,768]{1,0:T(4,128)}, u32[]{:S(2)}) copy-start(f32[3,768]{1,0:T(4,128)} %get-tuple-element.23) | copy-start | bytes 27652
  2036.2 138.6 %copy-start.9 = (f32[1,3,768]{2,1,0:T(4,128)S(1)}, f32[1,3,768]{2,1,0:T(4,128)}, u32[]{:S(2)}) copy-start(f32[1,3,768]{2,1,0:T(4,128)} %copy.84) | copy-start | bytes 27652
  2174.7 99.8 %copy-start.1 = (bf16[3,12,64,768]{3,2,1,0:T(8,128)(2,1)S(1)}, bf16[3,12,64,768]{3,2,1,0:T(8,128)(2,1)}, u32[]{:S(2)}) copy-start(bf16[3,12,64,768]{3,2,1,0:T(8,128)(2,1)} %param.17) | copy-start | bytes 10616836
where the time goes:
time: 2280 us; the launch traced here: 2270 us
  matrix products  1080 us (47%)
  blocking collectives  313 us (14%)
  local copies, waits for them, and re-layouts  308 us (14%)
  waiting for transfers between devices  301 us (13%)
  other arithmetic  263 us (12%)
    all_to_all x1, blocking collectives, local_block(): by_patch = lax.all_to_all(after_spatial, 'sp', 2, 1, tiled=True)  313 us
    all_to_all x1, waiting for transfers between devices, local_block(): by_frame = lax.all_to_all(after_temporal, 'sp', 1, 2, tiled=True)  301 us
    dot_general x1, matrix products, temporal_sublayer(): jnp.einsum('bqshd,bkshd->bshqk', qkv_all[0], qkv_all[1], preferred_elemen...  170 us
    dot_general x1, matrix products, temporal_sublayer(): jnp.einsum('btsc,jhdc->jbtshd', shifted, w_qkv, preferred_element_type=jn...  142 us
    squeeze x1, local copies, waits for them, and re-layouts, temporal_sublayer(): qkv_all[0]  140 us
    dot_general x1, matrix products, cross_mlp(): jnp.einsum('btsc,cf->btsf', normed, w_mlp_in, preferred_element_type=jnp....  139 us
    sub x1, other arithmetic, temporal_sublayer(): jax.nn.softmax(scores * head_dim ** (-0.5), axis=-1).astype(jnp.bfloat16)  112 us
    sub x1, other arithmetic, cross_mlp(): jax.nn.softmax(scores * head_dim ** (-0.5), axis=-1).astype(jnp.bfloat16)  103 us
  transfers between devices with their start and end apart: 1, of which 1 were waited for; matrix products, arithmetic and copies ran while one was open for 0% of the time, Pallas kernels for 0%

commit v1 on v0

v1 whole, which is shorter than its diff:
```python
import functools
import math

import jax
import jax.numpy as jnp
from jax import lax
from jax.experimental import pallas as pl
from jax.experimental.pallas import tpu as pltpu
from jax.sharding import PartitionSpec as P

LN_EPS = 1e-6
F32 = jnp.float32
BF16 = jnp.bfloat16
LANES = 128
NEG = -1e30
GELU_C = math.sqrt(2.0 / math.pi)
SPATIAL_CHUNKS = (((0, 12), (12, 12)), ((0, 24),), ((0, 24),))
SPLITS = (2, 1, 1)
VMEM_LIMIT = 60 * 1024 * 1024

NT = (((1,), (1,)), ((), ()))
NN = (((1,), (0,)), ((), ()))


def dot(lhs, rhs, dims=NN):
    return lax.dot_general(lhs, rhs, dims, preferred_element_type=F32)


def normalize(rows):
    centered = rows - jnp.mean(rows, axis=-1, keepdims=True)
    return centered * lax.rsqrt(jnp.mean(centered * centered, axis=-1, keepdims=True) + LN_EPS)


def pair_masks(rows):
    lane = lax.broadcasted_iota(jnp.int32, (rows, LANES), 1)
    return lane < LANES // 2


def split_pair(block, low):
    zero = jnp.zeros_like(block)
    return jnp.where(low, block, zero), jnp.where(low, zero, block)


def spatial_kernel(head_dim, frames, steps, me_ref, x_ref, old_ref, mod_ref, wqkv_ref, wout_ref, *rest):
    outs, (u_ref, qkv_ref, s_ref, p_ref, inv_ref, att_ref, res_ref) = rest[:4], rest[4:]
    tokens, width = x_ref.shape[2], x_ref.shape[3]
    chunk = 2 * LANES
    chunks = width // chunk
    units = [(f, p) for f in range(frames) for p in range(2)]
    coef = math.log2(math.e) * head_dim ** -0.5
    low = pair_masks(tokens)

    def enter():
        for f in range(frames):
            u = normalize(x_ref[0, f].astype(F32)) * (1.0 + mod_ref[0, 1:2, :]) + mod_ref[0, 0:1, :]
            u_ref[f * tokens:(f + 1) * tokens, :] = u.astype(BF16)

    def project(j, c):
        cols = slice(j * width + c * chunk, j * width + (c + 1) * chunk)
        qkv_ref[:, cols] = dot(u_ref[...], wqkv_ref[:, cols]).astype(BF16)

    def block(j, c, f, p):
        c0 = j * width + c * chunk + p * LANES
        return qkv_ref[f * tokens:(f + 1) * tokens, c0:c0 + LANES]

    def scores(c):
        for n, (f, p) in enumerate(units):
            q = block(0, c, f, p)
            for h, kh in enumerate(split_pair(block(1, c, f, p), low)):
                s_ref[c % 2, n, h] = dot(q, kh, NT)

    def softmax(c):
        for n in range(len(units)):
            inv = []
            for h in range(2):
                s = s_ref[c % 2, n, h]
                e = jnp.exp2((s - jnp.max(s, axis=-1, keepdims=True)) * coef)
                inv.append(1.0 / jnp.sum(e, axis=-1, keepdims=True))
                p_ref[c % 2, n, :, h * tokens:(h + 1) * tokens] = e.astype(BF16)
            inv_ref[c % 2, n] = jnp.where(low, inv[0], inv[1])

    def values(c):
        for n, (f, p) in enumerate(units):
            o = dot(p_ref[c % 2, n], jnp.concatenate(split_pair(block(2, c, f, p), low), axis=0))
            c0 = c * chunk + p * LANES
            att_ref[f * tokens:(f + 1) * tokens, c0:c0 + LANES] = (o * inv_ref[c % 2, n]).astype(BF16)

    def leave():
        part = tokens // 4
        for c in range(chunks):
            cols = slice(c * chunk, (c + 1) * chunk)
            branch = mod_ref[0, 2:3, cols] * dot(att_ref[...], wout_ref[:, cols])
            for f in range(frames):
                rows = slice(f * tokens, (f + 1) * tokens)
                res_ref[rows, cols] = (old_ref[0, f, :, cols].astype(F32) + branch[rows]).astype(BF16)
        for f in range(frames):
            for r in range(4):
                start = pl.multiple_of((me_ref[0] ^ r) * part, part)
                outs[r][f] = res_ref[pl.ds(f * tokens + start, part), :]

    def step(first, last):
        if not last:
            enter()
        for c in range(chunks + 1):
            if c < chunks:
                if not first:
                    scores(c)
                if not last:
                    project(0, c)
                    project(1, c)
            if c > 0:
                if not first:
                    softmax(c - 1)
                    values(c - 1)
                if not last:
                    project(2, c - 1)
        if not first:
            leave()

    i = pl.program_id(0)
    pl.when(i == 0)(lambda: step(True, False))
    pl.when(jnp.logical_and(i > 0, i < steps))(lambda: step(False, False))
    pl.when(i == steps)(lambda: step(False, True))


def spatial_call(me, latents, modulation, wqkv, wout, video, first, count, head_dim, frames=2):
    tokens, width = latents.shape[2:]
    part = tokens // 4
    rows = frames * tokens
    steps = count // frames
    base = first // frames
    act = (1, frames, tokens, width)
    grid_spec = pltpu.PrefetchScalarGridSpec(
        num_scalar_prefetch=1,
        grid=(steps + 1,),
        in_specs=[
            pl.BlockSpec(act, lambda i, me: (video, base + jnp.minimum(i, steps - 1), 0, 0)),
            pl.BlockSpec(act, lambda i, me: (video, base + jnp.maximum(i - 1, 0), 0, 0)),
            pl.BlockSpec((1, 6, width), lambda i, me: (video, 0, 0)),
            pl.BlockSpec(wqkv.shape, lambda i, me: (0, 0)),
            pl.BlockSpec(wout.shape, lambda i, me: (0, 0)),
        ],
        out_specs=[pl.BlockSpec((frames, part, width), lambda i, me: (jnp.maximum(i - 1, 0), 0, 0))] * 4,
        scratch_shapes=[
            pltpu.VMEM((rows, width), BF16),
            pltpu.VMEM((rows, 3 * width), BF16),
            pltpu.VMEM((2, 2 * frames, 2, tokens, tokens), F32),
            pltpu.VMEM((2, 2 * frames, tokens, 2 * tokens), BF16),
            pltpu.VMEM((2, 2 * frames, tokens, LANES), F32),
            pltpu.VMEM((rows, width), BF16),
            pltpu.VMEM((rows, width), BF16),
        ],
    )
    total = count * tokens
    flops = 2 * total * (4 * width * width + 2 * tokens * width)
    return pl.pallas_call(
        functools.partial(spatial_kernel, head_dim, frames, steps),
        grid_spec=grid_spec,
        out_shape=[jax.ShapeDtypeStruct((count, part, width), BF16)] * 4,
        compiler_params=pltpu.CompilerParams(vmem_limit_bytes=VMEM_LIMIT),
        cost_estimate=pl.CostEstimate(flops=flops, bytes_accessed=4 * total * width, transcendentals=0),
        name=f"spatial_{video}_{first}",
    )(me, latents, latents, modulation, wqkv, wout)


def temporal_kernel(head_dim, pieces, patches, splits, me_ref, *refs):
    ins, refs = refs[:4 * pieces], refs[4 * pieces:]
    pos, refs = refs[:4 * pieces], refs[4 * pieces:]
    mod_ref, wqkv_ref, wout_ref = refs[:3]
    outs = refs[3:3 + 4 * splits]
    xf_ref, h_ref, qkv_ref, att_ref, s_ref, p_ref, inv_ref, pos_ref = refs[3 + 4 * splits:]
    per, _, width = ins[0].shape
    steps = 4 * pieces * per
    pairs = width // LANES
    pad = LANES - steps
    coef = math.log2(math.e) * head_dim ** -0.5
    blocks = [slice(c, c + LANES) for c in range(0, width, LANES)]
    lane_in, lane_out = patches + 1, steps + 1
    for n, ref in enumerate(ins):
        pos_ref[n * per:(n + 1) * per, :] = pos[n][0]
        for f in range(per):
            for c, cols in enumerate(blocks):
                xf_ref[c, (n * per + f) * lane_in:(n * per + f) * lane_in + patches, :] = ref[f, :, cols].astype(F32)
    group = 4
    for g in range(0, patches, group):
        for p in range(g, g + group):
            for c, cols in enumerate(blocks):
                h = xf_ref[c, pl.ds(p, steps, stride=lane_in), :]
                h_ref[p * steps:(p + 1) * steps, cols] = h.astype(BF16)
                att_ref[p * steps:(p + 1) * steps, cols] = (h + pos_ref[:, cols]).astype(BF16)
        rows = slice(g * steps, (g + group) * steps)
        qkv_ref[rows, :] = dot(att_ref[rows, :], wqkv_ref[...]).astype(BF16)
    low = pair_masks(steps)
    gap = jnp.zeros((pad, LANES), BF16)
    live = lax.broadcasted_iota(jnp.int32, (steps, LANES), 1) < steps

    def rows_of(p):
        return slice(p * steps, (p + 1) * steps)

    def scores(p, slot):
        rows = rows_of(p)
        for q in range(pairs):
            c0 = q * LANES
            k0, k1 = split_pair(qkv_ref[rows, width + c0:width + c0 + LANES], low)
            s_ref[slot, q] = dot(qkv_ref[rows, c0:c0 + LANES], jnp.concatenate([k0, gap, k1, gap], axis=0), NT)

    def softmax(slot):
        for q in range(pairs):
            inv = []
            for h in range(2):
                cols = slice(h * LANES, (h + 1) * LANES)
                sh = jnp.where(live, s_ref[slot, q, :, cols], NEG)
                e = jnp.exp2((sh - jnp.max(sh, axis=-1, keepdims=True)) * coef)
                inv.append(1.0 / jnp.sum(e, axis=-1, keepdims=True))
                p_ref[slot, q, :, cols] = e.astype(BF16)
            inv_ref[slot, q] = jnp.where(low, inv[0], inv[1])

    def values(p, slot):
        rows = rows_of(p)
        for q in range(pairs):
            c0 = q * LANES
            v0, v1 = split_pair(qkv_ref[rows, 2 * width + c0:2 * width + c0 + LANES], low)
            o = dot(p_ref[slot, q], jnp.concatenate([v0, gap, v1, gap], axis=0))
            att_ref[rows, c0:c0 + LANES] = (o * inv_ref[slot, q]).astype(BF16)

    scores(0, 0)
    scores(1, 1)
    softmax(0)

    for p in range(patches - 2):
        values(p, p % 2)
        softmax((p + 1) % 2)
        scores(p + 2, p % 2)
    values(patches - 2, 0)
    softmax(1)
    values(patches - 1, 1)
    wide = 2 * LANES
    for g in range(0, patches, group):
        rows = slice(g * steps, (g + group) * steps)
        for d in range(0, width, wide):
            branch = dot(att_ref[rows, :], wout_ref[:, d:d + wide])
            h2 = h_ref[rows, d:d + wide].astype(F32) + mod_ref[0, 2:3, d:d + wide] * branch
            for k in range(group):
                dst = slice((g + k) * lane_out, (g + k) * lane_out + steps)
                xf_ref[d // LANES, dst, :] = h2[k * steps:(k + 1) * steps, :LANES]
                xf_ref[d // LANES + 1, dst, :] = h2[k * steps:(k + 1) * steps, LANES:]
    span = pieces * per // splits
    for n in range(4 * pieces):
        for f in range(per):
            at = n // 4 * per + f
            ref = outs[at // span * 4 + n % 4]
            for c, cols in enumerate(blocks):
                ref[at % span, :, cols] = xf_ref[c, pl.ds(n * per + f, patches, stride=lane_out), :].astype(BF16)


def temporal_call(me, pieces, pos, modulation, wqkv, wout, video, splits, head_dim, patches=16):
    per, part, width = pieces[0].shape
    count = len(pieces) // 4
    steps = len(pieces) * per
    rows = steps * patches
    span = count * per // splits
    total = steps * part
    flops = 2 * total * (4 * width * width + 4 * LANES * width)
    pos = pos.reshape(4 * count, per, width)
    pos_spec = lambda r, h: pl.BlockSpec((1, per, width), lambda i, me: ((me[0] ^ r) * count + h, 0, 0))
    grid_spec = pltpu.PrefetchScalarGridSpec(
        num_scalar_prefetch=1,
        grid=(part // patches,),
        in_specs=[pl.BlockSpec((per, patches, width), lambda i, me: (0, i, 0))] * len(pieces)
        + [pos_spec(r, h) for h in range(count) for r in range(4)]
        + [
            pl.BlockSpec((1, 6, width), lambda i, me: (video, 0, 0)),
            pl.BlockSpec(wqkv.shape, lambda i, me: (0, 0)),
            pl.BlockSpec(wout.shape, lambda i, me: (0, 0)),
        ],
        out_specs=[pl.BlockSpec((span, patches, width), lambda i, me: (0, i, 0))] * (4 * splits),
        scratch_shapes=[
            pltpu.VMEM((width // LANES, rows + LANES, LANES), F32),
            pltpu.VMEM((rows, width), BF16),
            pltpu.VMEM((rows, 3 * width), BF16),
            pltpu.VMEM((rows, width), BF16),
            pltpu.VMEM((2, width // LANES, steps, 2 * LANES), F32),
            pltpu.VMEM((2, width // LANES, steps, 2 * LANES), BF16),
            pltpu.VMEM((2, width // LANES, steps, LANES), F32),
            pltpu.VMEM((steps, width), F32),
        ],
    )
    return pl.pallas_call(
        functools.partial(temporal_kernel, head_dim, count, patches, splits),
        grid_spec=grid_spec,
        out_shape=[jax.ShapeDtypeStruct((span, part, width), BF16)] * (4 * splits),
        compiler_params=pltpu.CompilerParams(vmem_limit_bytes=VMEM_LIMIT),
        cost_estimate=pl.CostEstimate(flops=flops, bytes_accessed=4 * total * width, transcendentals=0),
        name=f"temporal_{video}",
    )(me, *pieces, *([pos] * len(pieces)), modulation, wqkv, wout)


def cross_kernel(head_dim, frames, text_len, steps, me_ref, *refs):
    ins = refs[:4]
    mod_ref, kk_ref, vv_ref, wq_ref, wo_ref, win_ref, wmid_ref = refs[4:11]
    out_ref, h_ref, q_ref, s_ref, p_ref, inv_ref, att_ref, new_ref, h3_ref, n_ref, g_ref = refs[-11:]
    part, width = ins[0].shape[1:]
    tokens = 4 * part
    rows = frames * tokens
    hidden = win_ref.shape[1]
    pairs = width // LANES
    span = hidden // pairs
    wide = 2 * LANES
    coef = math.log2(math.e) * head_dim ** -0.5
    low = pair_masks(rows)
    live = lax.broadcasted_iota(jnp.int32, (rows, LANES), 1) < text_len

    def enter():
        for f in range(frames):
            for r in range(4):
                h_ref[f * tokens + r * part:f * tokens + (r + 1) * part, :] = ins[r][f]
        q_ref[...] = dot(h_ref[...], wq_ref[...]).astype(BF16)

    def scores(p):
        s_ref[p % 2] = dot(q_ref[:, p * LANES:(p + 1) * LANES], kk_ref[0, p], NT)

    def softmax(p):
        inv = []
        for h in range(2):
            cols = slice(h * LANES, (h + 1) * LANES)
            sh = jnp.where(live, s_ref[p % 2, :, cols], NEG)
            e = jnp.exp2((sh - jnp.max(sh, axis=-1, keepdims=True)) * coef)
            inv.append(1.0 / jnp.sum(e, axis=-1, keepdims=True))
            p_ref[p % 2, :, cols] = e.astype(BF16)
        inv_ref[p % 2] = jnp.where(low, inv[0], inv[1])

    def values(p):
        o = dot(p_ref[p % 2], vv_ref[0, p])
        att_ref[:, p * LANES:(p + 1) * LANES] = (o * inv_ref[p % 2]).astype(BF16)

    def expand(p):
        cols = slice(p * span, (p + 1) * span)
        a = dot(n_ref[...], win_ref[:, cols])
        t = jnp.tanh(a * (GELU_C + (GELU_C * 0.044715) * (a * a)))
        half = 0.5 * a
        g_ref[:, cols] = (half + half * t).astype(BF16)

    def attend_out():
        for d in range(0, width, wide):
            cols = slice(d, d + wide)
            new_ref[:, cols] = (h_ref[:, cols].astype(F32) + dot(att_ref[...], wo_ref[:, cols])).astype(BF16)

    def norm():
        n_ref[...] = (normalize(new_ref[...].astype(F32)) * (1.0 + mod_ref[0, 4:5, :]) + mod_ref[0, 3:4, :]).astype(BF16)

    def contract():
        for d in range(0, width, wide):
            cols = slice(d, d + wide)
            y = (h3_ref[:, cols].astype(F32) + mod_ref[0, 5:6, cols] * dot(g_ref[...], wmid_ref[:, cols])).astype(BF16)
            for f in range(frames):
                for r in range(4):
                    start = pl.multiple_of((me_ref[0] ^ r) * part, part)
                    out_ref[0, f, pl.ds(start, part), cols] = y[f * tokens + r * part:f * tokens + (r + 1) * part]

    def step(first, last):
        if not last:
            enter()
            scores(0)
        for p in range(pairs):
            if not last and p + 1 < pairs:
                scores(p + 1)
            if not first:
                expand(p)
            if not last:
                softmax(p)
                values(p)
        if not last:
            attend_out()
            norm()
        if not first:
            contract()
        if not last:
            h3_ref[...] = new_ref[...]

    i = pl.program_id(0)
    pl.when(i == 0)(lambda: step(True, False))
    pl.when(jnp.logical_and(i > 0, i < steps))(lambda: step(False, False))
    pl.when(i == steps)(lambda: step(False, True))


def cross_call(me, pieces, modulation, kk, vv, wq, wo, win, wmid, prev, out_shape, video, first, text_len, head_dim, frames=2):
    per, part, width = pieces[0].shape
    rows = frames * 4 * part
    hidden = win.shape[1]
    steps = per // frames
    base = first // frames
    whole = lambda a: pl.BlockSpec(a.shape, lambda i, me: (0, 0))
    in_specs = [pl.BlockSpec((frames, part, width), lambda i, me: (jnp.minimum(i, steps - 1), 0, 0))] * 4 + [
        pl.BlockSpec((1, 6, width), lambda i, me: (video, 0, 0)),
        pl.BlockSpec((1,) + kk.shape[1:], lambda i, me: (video, 0, 0, 0)),
        pl.BlockSpec((1,) + vv.shape[1:], lambda i, me: (video, 0, 0, 0)),
        whole(wq), whole(wo), whole(win), whole(wmid),
    ]
    args = [me, *pieces, modulation, kk, vv, wq, wo, win, wmid]
    aliases = {}
    if prev is not None:
        in_specs.append(pl.BlockSpec(memory_space=pl.ANY))
        aliases = {len(args): 0}
        args.append(prev)
    grid_spec = pltpu.PrefetchScalarGridSpec(
        num_scalar_prefetch=1,
        grid=(steps + 1,),
        in_specs=in_specs,
        out_specs=pl.BlockSpec((1, frames, 4 * part, width), lambda i, me: (video, base + jnp.maximum(i - 1, 0), 0, 0)),
        scratch_shapes=[
            pltpu.VMEM((rows, width), BF16),
            pltpu.VMEM((rows, width), BF16),
            pltpu.VMEM((2, rows, 2 * LANES), F32),
            pltpu.VMEM((2, rows, 2 * LANES), BF16),
            pltpu.VMEM((2, rows, LANES), F32),
            pltpu.VMEM((rows, width), BF16),
            pltpu.VMEM((rows, width), BF16),
            pltpu.VMEM((rows, width), BF16),
            pltpu.VMEM((rows, width), BF16),
            pltpu.VMEM((rows, hidden), BF16),
        ],
    )
    total = per * 4 * part
    flops = 2 * total * (2 * width * width + 4 * LANES * width + 2 * width * hidden)
    return pl.pallas_call(
        functools.partial(cross_kernel, head_dim, frames, text_len, steps),
        grid_spec=grid_spec,
        out_shape=jax.ShapeDtypeStruct(out_shape, BF16),
        input_output_aliases=aliases,
        compiler_params=pltpu.CompilerParams(vmem_limit_bytes=VMEM_LIMIT),
        cost_estimate=pl.CostEstimate(flops=flops, bytes_accessed=4 * total * width, transcendentals=0),
        name=f"cross_{video}_{first}",
    )(*args)


def text_kernel(ctx_ref, wkv_ref, kk_ref, vv_ref):
    length, width = ctx_ref.shape[1:]
    kv = dot(ctx_ref[0], wkv_ref[...], NT)
    kv = jnp.concatenate([kv, jnp.zeros((LANES - length, 2 * width), F32)], axis=0).astype(BF16)
    low = pair_masks(LANES)
    for p in range(width // LANES):
        for ref, c0 in ((kk_ref, p * LANES), (vv_ref, width + p * LANES)):
            for h, half in enumerate(split_pair(kv[:, c0:c0 + LANES], low)):
                ref[0, p, h * LANES:(h + 1) * LANES, :] = half


def text_blocks(text_ctx, w_kv):
    videos, length, width = text_ctx.shape
    block = (1, width // LANES, 2 * LANES, LANES)
    return pl.pallas_call(
        text_kernel,
        grid=(videos,),
        in_specs=[pl.BlockSpec((1, length, width), lambda b: (b, 0, 0)), pl.BlockSpec(w_kv.shape, lambda b: (0, 0))],
        out_specs=[pl.BlockSpec(block, lambda b: (b, 0, 0, 0))] * 2,
        out_shape=[jax.ShapeDtypeStruct((videos,) + block[1:], BF16)] * 2,
        compiler_params=pltpu.CompilerParams(vmem_limit_bytes=VMEM_LIMIT),
        cost_estimate=pl.CostEstimate(flops=4 * videos * LANES * width * width, bytes_accessed=w_kv.size * 2, transcendentals=0),
        name="text",
    )(text_ctx, w_kv)


def solution(mesh):
    act_spec = P('dp', 'sp', None, None)
    row_spec = P('dp', None, None)
    rep_two = P(None, None)
    rep_three = P(None, None, None)
    rep_four = P(None, None, None, None)
    in_specs = (act_spec, row_spec, row_spec, rep_two, rep_four, rep_three, rep_four, rep_three, rep_three, rep_four, rep_three, rep_two, rep_two)
    def exchange(parts):
        return [parts[0]] + [lax.ppermute(parts[r], 'sp', [(i, i ^ r) for i in range(4)]) for r in range(1, 4)]

    def local_block(latents, text_ctx, modulation, pos_temporal, w_qkv_spatial, w_out_spatial, w_qkv_temporal, w_out_temporal, w_query_cross, w_kv_cross, w_out_cross, w_mlp_in, w_mlp_out):
        videos, frames, tokens, width = latents.shape
        head_dim = w_out_spatial.shape[1]
        index = lax.axis_index('sp')
        me = index.astype(jnp.int32)[None]
        flat_in = lambda w: w.reshape(-1, width).T
        flat_out = lambda w: w.reshape(width, width)
        wqkv_s, wqkv_t, wq_c = flat_in(w_qkv_spatial), flat_in(w_qkv_temporal), flat_in(w_query_cross)
        wo_s, wo_t, wo_c = flat_out(w_out_spatial), flat_out(w_out_temporal), flat_out(w_out_cross)
        kk, vv = text_blocks(text_ctx, w_kv_cross.reshape(-1, width))
        gathered = []
        for b in range(videos):
            pieces = []
            for first, count in SPATIAL_CHUNKS[b]:
                pieces += exchange(spatial_call(me, latents, modulation, wqkv_s, wo_s, b, first, count, head_dim))
            gathered.append(pieces)
        returned = []
        for b in range(videos):
            splits = SPLITS[b]
            parts = temporal_call(me, gathered[b], pos_temporal, modulation, wqkv_t, wo_t, b, splits, head_dim)
            returned.append([exchange(parts[4 * n:4 * n + 4]) for n in range(splits)])
        y = None
        for b in range(videos):
            for n, pieces in enumerate(returned[b]):
                y = cross_call(me, pieces, modulation, kk, vv, wq_c, wo_c, w_mlp_in, w_mlp_out, y, latents.shape, b, n * frames // SPLITS[b], text_ctx.shape[1], head_dim)
        return y

    return jax.shard_map(local_block, mesh=mesh, in_specs=in_specs, out_specs=act_spec, check_vma=False)
```

time: 2280 us -> 827 us (0.36)
  matrix products: 1080 us -> 0 us
  Pallas kernels: 0 us -> 734 us
  blocking collectives: 313 us -> 0 us
  local copies, waits for them, and re-layouts: 308 us -> 14 us
  other arithmetic: 263 us -> 0 us
  waiting for transfers between devices: 301 us -> 53.4 us
    dot_general x11 -> x0, matrix products: 979 us -> none  [the longest x1 170 us: temporal_sublayer(): jnp.einsum('bqshd,bkshd->bshqk', qkv_all[0], qkv_all[1], preferred_elemen...]
    pallas_call x0 -> x12, Pallas kernels: none -> 734 us  [the longest x4 350 us: cross_call(): pl.pallas_call(functools.partial(cross_kernel, head_dim, frames, text_len...]
    all_to_all x1 -> x0, blocking collectives: 313 us -> none  [local_block(): by_patch = lax.all_to_all(after_spatial, 'sp', 2, 1, tiled=True)]
    all_to_all x1 -> x0, waiting for transfers between devices: 301 us -> none  [local_block(): by_frame = lax.all_to_all(after_temporal, 'sp', 1, 2, tiled=True)]
    sub x2 -> x0, other arithmetic: 215 us -> none  [the longest x1 112 us: temporal_sublayer(): jax.nn.softmax(scores * head_dim ** (-0.5), axis=-1).astype(jnp.bfloat16)]
    squeeze x2 -> x0, local copies, waits for them, and re-layouts: 141 us -> none  [the longest x1 140 us: temporal_sublayer(): qkv_all[0]]
    sub x1 -> x0, matrix products: 100 us -> none  [spatial_sublayer(): jax.nn.softmax(scores * head_dim ** (-0.5), axis=-1).astype(jnp.bfloat16)]
    dot_general x1 -> x0, local copies, waits for them, and re-layouts: 88.6 us -> none  [temporal_sublayer(): jnp.einsum('bshqk,bkshd->bqshd', attn_probs, qkv_all[2], preferred_elemen...]
  transfers between devices with their start and end apart: 1 -> 24, of which waited for: 1 -> 2; matrix products, arithmetic and copies ran while one was open for 0% -> 1% of each run, Pallas kernels for 0% -> 71%
where the time goes in v1:
time: 827 us; the launch traced here: 820 us
  Pallas kernels  734 us (89%)
  waiting for transfers between devices  53.4 us (6%)
  starting transfers between devices  18.2 us (2%)
  local copies, waits for them, and re-layouts  14 us (2%)
    pallas_call x4, Pallas kernels, cross_call(): pl.pallas_call(functools.partial(cross_kernel, head_dim, frames, text_len...  350 us
    pallas_call x4, Pallas kernels, spatial_call(): pl.pallas_call(functools.partial(spatial_kernel, head_dim, frames, steps)...  194 us
    pallas_call x3, Pallas kernels, temporal_call(): pl.pallas_call(functools.partial(temporal_kernel, head_dim, count, patche...  185 us
    ppermute x24, waiting for transfers between devices, exchange(): lax.ppermute(parts[r], 'sp', [(i, i ^ r) for i in range(4)])  53.4 us
    ppermute x24, starting transfers between devices, exchange(): lax.ppermute(parts[r], 'sp', [(i, i ^ r) for i in range(4)])  18.2 us
  transfers between devices with their start and end apart: 24, of which 2 were waited for; matrix products, arithmetic and copies ran while one was open for 1% of the time, Pallas kernels for 71%

profile of v1, /device:TPU:0, one launch (start us, length us, event | category | flops | bytes accessed | tf_op | source)
XLA Modules:
  0.0 820.0 jit_solution(11819698647972194708)
XLA Ops:
  0.0 5.7 copy.20
  5.7 33.7 %spatial_0_0.1 = (bf16[12,64,768]{2,1,0:T(8,128)(2,1)}, bf16[12,64,768]{2,1,0:T(8,128)(2,1)}, bf16[12,64,768]{2,1,0:T(8,128)(2,1)}, bf16[12,64,768]{2,1,0:T(8,128)(2,1)}) custom-call(s32[1]{0:T(128)} %bitcast.me_ref, bf16[3,24,256,768]{3,2,1,0:T(8,128)(2,1)} %old_ref.7, bf16[3,24,256,768]{3,2,1,0:T(8,128)(2,1)} %old_ref.7, f32[3,6,768]{2,1,0:T(8,128)} %refs_4_.7, ...), custom_call_target="tpu_custom_call" | custom-call | flops 16911433728 | bytes 9437184 | tf_op jit(solution)/shard_map/spatial_0_0/pallas_call | solution.py:156
  39.4 0.9 collective-permute-start.12
  40.3 2.5 collective-permute-start.13
  42.8 0.1 collective-permute-start.14
  42.9 33.9 %spatial_0_12.1 = (bf16[12,64,768]{2,1,0:T(8,128)(2,1)}, bf16[12,64,768]{2,1,0:T(8,128)(2,1)}, bf16[12,64,768]{2,1,0:T(8,128)(2,1)}, bf16[12,64,768]{2,1,0:T(8,128)(2,1)}) custom-call(s32[1]{0:T(128)} %bitcast.me_ref, bf16[3,24,256,768]{3,2,1,0:T(8,128)(2,1)} %old_ref.7, bf16[3,24,256,768]{3,2,1,0:T(8,128)(2,1)} %old_ref.7, f32[3,6,768]{2,1,0:T(8,128)} %refs_4_.7, ...), custom_call_target="tpu_custom_call" | custom-call | flops 16911433728 | bytes 9437184 | tf_op jit(solution)/shard_map/spatial_0_12/pallas_call | solution.py:156
  76.7 0.1 collective-permute-start.15
  76.9 1.9 collective-permute-start.16
  78.8 0.0 collective-permute-done.12.refs_1_
  78.8 1.0 copy-done.5
  79.8 0.0 collective-permute-start.17
  79.8 63.5 %spatial_1_0.1 = (bf16[24,64,768]{2,1,0:T(8,128)(2,1)}, bf16[24,64,768]{2,1,0:T(8,128)(2,1)}, bf16[24,64,768]{2,1,0:T(8,128)(2,1)}, bf16[24,64,768]{2,1,0:T(8,128)(2,1)}) custom-call(s32[1]{0:T(128)} %bitcast.me_ref, bf16[3,24,256,768]{3,2,1,0:T(8,128)(2,1)} %old_ref.7, bf16[3,24,256,768]{3,2,1,0:T(8,128)(2,1)} %old_ref.7, f32[3,6,768]{2,1,0:T(8,128)} %refs_4_.7, ...), custom_call_target="tpu_custom_call" | custom-call | flops 33822867456 | bytes 18874368 | tf_op jit(solution)/shard_map/spatial_1_0/pallas_call | solution.py:156
  143.3 4.0 copy.21
  147.3 1.7 reshape.36.refs_8_.refs_9_.refs_10_.refs_11_.refs_12_.refs_13_.refs_14_.refs_15_
  149.0 0.0 collective-permute-done.13.refs_2_
  149.0 0.2 collective-permute-start.6
  149.3 0.0 collective-permute-done.14.refs_3_
  149.3 1.9 collective-permute-start.7
  151.2 0.0 collective-permute-done.15.refs_5_
  151.2 0.0 collective-permute-done.16.refs_6_
  151.2 0.0 collective-permute-done.17.refs_7_
  151.2 62.1 %temporal_0.1 = (bf16[12,64,768]{2,1,0:T(8,128)(2,1)}, bf16[12,64,768]{2,1,0:T(8,128)(2,1)}, bf16[12,64,768]{2,1,0:T(8,128)(2,1)}, bf16[12,64,768]{2,1,0:T(8,128...) custom-call(s32[1]{0:T(128)} %bitcast.me_ref, ...), custom_call_target="tpu_custom_call" | custom-call | flops 33822867456 | bytes 18874368 | tf_op jit(solution)/shard_map/temporal_0/pallas_call | solution.py:288
  213.3 0.0 collective-permute-start.21
  213.4 0.1 collective-permute-start.22
  213.5 1.7 collective-permute-start.23
  215.2 62.9 %spatial_2_0.1 = (bf16[24,64,768]{2,1,0:T(8,128)(2,1)}, bf16[24,64,768]{2,1,0:T(8,128)(2,1)}, bf16[24,64,768]{2,1,0:T(8,128)(2,1)}, bf16[24,64,768]{2,1,0:T(8,128)(2,1)}) custom-call(s32[1]{0:T(128)} %bitcast.me_ref, bf16[3,24,256,768]{3,2,1,0:T(8,128)(2,1)} %old_ref.7, bf16[3,24,256,768]{3,2,1,0:T(8,128)(2,1)} %old_ref.7, f32[3,6,768]{2,1,0:T(8,128)} %refs_4_.7, ...), custom_call_target="tpu_custom_call" | custom-call | flops 33822867456 | bytes 18874368 | tf_op jit(solution)/shard_map/spatial_2_0/pallas_call | solution.py:156
  278.1 1.5 copy.22
  279.6 5.4 text.1
  285.0 0.0 collective-permute-done.21.refs_1_
  285.0 0.1 collective-permute-start.8
  285.1 0.0 collective-permute-done.22.refs_2_
  285.1 0.4 collective-permute-start
  285.5 0.0 collective-permute-done.23.refs_3_
  285.5 1.7 collective-permute-start.1
  287.2 60.7 %cross_0_0.1.refs_11_ = bf16[3,24,256,768]{3,2,1,0:T(8,128)(2,1)} custom-call(s32[1]{0:T(128)} %bitcast.me_ref, bf16[12,64,768]{2,1,0:T(8,128)(2,1)} %get-tuple-element.69.refs_0_, bf16[12,64,768]{2,1,0:T(8,128)(2,1)} %collective-permute-done.21.refs_1_, bf16[12,64,768]{2,1,0:T(8,128)(2,1)} %collective-permute-done.22.refs_2_, ...), custom_call_target="tpu_custom_call" | custom-call | flops 38654705664 | bytes 9437184 | tf_op jit(solution)/shard_map/cross_0_0/pallas_call | solution.py:425
  347.9 0.0 collective-permute-done.6.refs_1_
  347.9 0.0 collective-permute-start.2
  347.9 0.0 collective-permute-done.7.refs_2_
  347.9 0.4 collective-permute-start.18
  348.4 0.0 collective-permute-done.8.refs_3_
  348.4 1.7 collective-permute-start.19
  350.1 61.2 %temporal_1.1 = (bf16[24,64,768]{2,1,0:T(8,128)(2,1)}, bf16[24,64,768]{2,1,0:T(8,128)(2,1)}, bf16[24,64,768]{2,1,0:T(8,128)(2,1)}, bf16[24,64,768]{2,1,0:T(8,128)(2,1)}) custom-call(s32[1]{0:T(128)} %bitcast.me_ref, bf16[24,64,768]{2,1,0:T(8,128)(2,1)} %get-tuple-element.49.refs_0_, bf16[24,64,768]{2,1,0:T(8,128)(2,1)} %copy-done.2, ...), custom_call_target="tpu_custom_call" | custom-call | flops 33822867456 | bytes 18874368 | tf_op jit(solution)/shard_map/temporal_1/pallas_call | solution.py:288
  411.2 0.0 collective-permute-done.refs_1_
  411.2 0.0 collective-permute-start.20
  411.3 0.0 collective-permute-done.1.refs_2_
  411.3 1.4 collective-permute-start.10
  412.6 26.6 %collective-permute-done.2.refs_3_ = bf16[24,64,768]{2,1,0:T(8,128)(2,1)} collective-permute-done((bf16[24,64,768]{2,1,0:T(8,128)(2,1)}, bf16[24,64,768]{2,1,0:T(8,128)(2,1)}, u32[]{:S(2)}, u32[]{:S(2)}) %collective-permute-start.2) | collective-permute-done | bytes 2359328 | tf_op jit(solution)/shard_map/ppermute | solution.py:470
  439.2 0.6 collective-permute-start.11
  439.8 61.3 %temporal_2.1 = (bf16[24,64,768]{2,1,0:T(8,128)(2,1)}, bf16[24,64,768]{2,1,0:T(8,128)(2,1)}, bf16[24,64,768]{2,1,0:T(8,128)(2,1)}, bf16[24,64,768]{2,1,0:T(8,128)(2,1)}) custom-call(s32[1]{0:T(128)} %bitcast.me_ref, bf16[24,64,768]{2,1,0:T(8,128)(2,1)} %get-tuple-element.39.refs_0_, bf16[24,64,768]{2,1,0:T(8,128)(2,1)} %collective-permute-done.refs_1_, ...), custom_call_target="tpu_custom_call" | custom-call | flops 33822867456 | bytes 18874368 | tf_op jit(solution)/shard_map/temporal_2/pallas_call | solution.py:288
  501.1 0.0 collective-permute-done.18.refs_1_
  501.1 0.2 collective-permute-start.9
  501.4 0.0 collective-permute-done.19.refs_2_
  501.4 0.3 collective-permute-start.3
  501.7 0.0 collective-permute-done.20.refs_3_
  501.7 1.8 collective-permute-start.4
  503.5 60.5 %cross_0_12.1.refs_11_ = bf16[3,24,256,768]{3,2,1,0:T(8,128)(2,1)} custom-call(s32[1]{0:T(128)} %bitcast.me_ref, bf16[12,64,768]{2,1,0:T(8,128)(2,1)} %get-tuple-element.65.refs_0_, bf16[12,64,768]{2,1,0:T(8,128)(2,1)} %collective-permute-done.18.refs_1_, bf16[12,64,768]{2,1,0:T(8,128)(2,1)} %collective-permute-done.19.refs_2_, ...), custom_call_target="tpu_custom_call", output_to_operand_aliasing={{}: (12, {})} | custom-call | flops 38654705664 | bytes 9437184 | tf_op jit(solution)/shard_map/cross_0_12/pallas_call | solution.py:425
  564.1 0.0 collective-permute-done.10.refs_2_
  564.1 0.0 collective-permute-start.5
  564.1 26.8 %collective-permute-done.11.refs_3_ = bf16[24,64,768]{2,1,0:T(8,128)(2,1)} collective-permute-done((bf16[24,64,768]{2,1,0:T(8,128)(2,1)}, bf16[24,64,768]{2,1,0:T(8,128)(2,1)}, u32[]{:S(2)}, u32[]{:S(2)}) %collective-permute-start.11) | collective-permute-done | bytes 2359328 | tf_op jit(solution)/shard_map/ppermute | solution.py:470
  590.9 0.0 collective-permute-done.9.refs_1_
  590.9 114.3 %cross_1_0.1.refs_11_ = bf16[3,24,256,768]{3,2,1,0:T(8,128)(2,1)} custom-call(s32[1]{0:T(128)} %bitcast.me_ref, bf16[24,64,768]{2,1,0:T(8,128)(2,1)} %get-tuple-element.53.refs_0_, bf16[24,64,768]{2,1,0:T(8,128)(2,1)} %collective-permute-done.9.refs_1_, bf16[24,64,768]{2,1,0:T(8,128)(2,1)} %collective-permute-done.10.refs_2_, ...), custom_call_target="tpu_custom_call", output_to_operand_aliasing={{}: (12, {})} | custom-call | flops 77309411328 | bytes 18874368 | tf_op jit(solution)/shard_map/cross_1_0/pallas_call | solution.py:425
  705.2 0.0 collective-permute-done.3.refs_1_
  705.2 0.0 collective-permute-done.4.refs_2_
  705.2 114.4 %cross_2_0.1 = bf16[3,24,256,768]{3,2,1,0:T(8,128)(2,1)} custom-call(s32[1]{0:T(128)} %bitcast.me_ref, bf16[24,64,768]{2,1,0:T(8,128)(2,1)} %get-tuple-element.43.refs_0_, bf16[24,64,768]{2,1,0:T(8,128)(2,1)} %collective-permute-done.3.refs_1_, bf16[24,64,768]{2,1,0:T(8,128)(2,1)} %collective-permute-done.4.refs_2_, ...), custom_call_target="tpu_custom_call", output_to_operand_aliasing={{}: (12, {})} | custom-call | flops 77309411328 | bytes 18874368 | tf_op jit(solution)/shard_map/cross_2_0/pallas_call | solution.py:425
  (12 shorter events, 0.0 us)
Async XLA Ops:
  39.4 39.4 %collective-permute-start.12 = (bf16[12,64,768]{2,1,0:T(8,128)(2,1)}, bf16[12,64,768]{2,1,0:T(8,128)(2,1)S(1)}, u32[]{:S(2)}, u32[]{:S(2)}) collective-permute-start(bf16[12,64,768]{2,1,0:T(8,128)(2,1)} %get-tuple-element.58), channel_id=1, source_target_pairs={{0,1},{1,0},{2,3},{3,2},{4,5},{5,4},{6,7},{7,6}} | collective-permute-start | bytes 3538952 | tf_op jit(solution)/shard_map/ppermute | solution.py:470
  40.3 108.8 %collective-permute-start.13 = (bf16[12,64,768]{2,1,0:T(8,128)(2,1)}, bf16[12,64,768]{2,1,0:T(8,128)(2,1)}, u32[]{:S(2)}, u32[]{:S(2)}) collective-permute-start(bf16[12,64,768]{2,1,0:T(8,128)(2,1)} %get-tuple-element.59), channel_id=1, source_target_pairs={{0,2},{1,3},{2,0},{3,1},{4,6},{5,7},{6,4},{7,5}} | collective-permute-start | bytes 3538952 | tf_op jit(solution)/shard_map/ppermute | solution.py:470
  42.8 106.5 %collective-permute-start.14 = (bf16[12,64,768]{2,1,0:T(8,128)(2,1)}, bf16[12,64,768]{2,1,0:T(8,128)(2,1)}, u32[]{:S(2)}, u32[]{:S(2)}) collective-permute-start(bf16[12,64,768]{2,1,0:T(8,128)(2,1)} %get-tuple-element.60), channel_id=1, source_target_pairs={{0,3},{1,2},{2,1},{3,0},{4,7},{5,6},{6,5},{7,4}} | collective-permute-start | bytes 3538952 | tf_op jit(solution)/shard_map/ppermute | solution.py:470
  76.7 74.4 %collective-permute-start.15 = (bf16[12,64,768]{2,1,0:T(8,128)(2,1)}, bf16[12,64,768]{2,1,0:T(8,128)(2,1)}, u32[]{:S(2)}, u32[]{:S(2)}) collective-permute-start(bf16[12,64,768]{2,1,0:T(8,128)(2,1)} %get-tuple-element.62), channel_id=1, source_target_pairs={{0,1},{1,0},{2,3},{3,2},{4,5},{5,4},{6,7},{7,6}} | collective-permute-start | bytes 3538952 | tf_op jit(solution)/shard_map/ppermute | solution.py:470
  76.9 74.3 %collective-permute-start.16 = (bf16[12,64,768]{2,1,0:T(8,128)(2,1)}, bf16[12,64,768]{2,1,0:T(8,128)(2,1)}, u32[]{:S(2)}, u32[]{:S(2)}) collective-permute-start(bf16[12,64,768]{2,1,0:T(8,128)(2,1)} %get-tuple-element.63), channel_id=1, source_target_pairs={{0,2},{1,3},{2,0},{3,1},{4,6},{5,7},{6,4},{7,5}} | collective-permute-start | bytes 3538952 | tf_op jit(solution)/shard_map/ppermute | solution.py:470
  78.8 1.0 copy-start.5
  79.8 71.4 %collective-permute-start.17 = (bf16[12,64,768]{2,1,0:T(8,128)(2,1)}, bf16[12,64,768]{2,1,0:T(8,128)(2,1)}, u32[]{:S(2)}, u32[]{:S(2)}) collective-permute-start(bf16[12,64,768]{2,1,0:T(8,128)(2,1)} %get-tuple-element.64), channel_id=1, source_target_pairs={{0,3},{1,2},{2,1},{3,0},{4,7},{5,6},{6,5},{7,4}} | collective-permute-start | bytes 3538952 | tf_op jit(solution)/shard_map/ppermute | solution.py:470
  79.8 63.5 %copy-start = (bf16[3,12,64,768]{3,2,1,0:T(8,128)(2,1)S(1)}, bf16[3,12,64,768]{3,2,1,0:T(8,128)(2,1)}, u32[]{:S(2)}) copy-start(bf16[3,12,64,768]{3,2,1,0:T(8,128)(2,1)} %param.19) | copy-start | bytes 10616836
  149.0 198.8 %collective-permute-start.6 = (bf16[24,64,768]{2,1,0:T(8,128)(2,1)}, bf16[24,64,768]{2,1,0:T(8,128)(2,1)S(1)}, u32[]{:S(2)}, u32[]{:S(2)}) collective-permute-start(bf16[24,64,768]{2,1,0:T(8,128)(2,1)} %get-tuple-element.50), channel_id=1, source_target_pairs={{0,1},{1,0},{2,3},{3,2},{4,5},{5,4},{6,7},{7,6}} | collective-permute-start | bytes 7077896 | tf_op jit(solution)/shard_map/ppermute | solution.py:470
  149.3 198.6 %collective-permute-start.7 = (bf16[24,64,768]{2,1,0:T(8,128)(2,1)}, bf16[24,64,768]{2,1,0:T(8,128)(2,1)}, u32[]{:S(2)}, u32[]{:S(2)}) collective-permute-start(bf16[24,64,768]{2,1,0:T(8,128)(2,1)} %get-tuple-element.51), channel_id=1, source_target_pairs={{0,2},{1,3},{2,0},{3,1},{4,6},{5,7},{6,4},{7,5}} | collective-permute-start | bytes 7077896 | tf_op jit(solution)/shard_map/ppermute | solution.py:470
  213.3 71.7 %collective-permute-start.21 = (bf16[12,64,768]{2,1,0:T(8,128)(2,1)}, bf16[12,64,768]{2,1,0:T(8,128)(2,1)}, u32[]{:S(2)}, u32[]{:S(2)}) collective-permute-start(bf16[12,64,768]{2,1,0:T(8,128)(2,1)} %get-tuple-element.70), channel_id=1, source_target_pairs={{0,1},{1,0},{2,3},{3,2},{4,5},{5,4},{6,7},{7,6}} | collective-permute-start | bytes 3538952 | tf_op jit(solution)/shard_map/ppermute | solution.py:470
  213.4 71.8 %collective-permute-start.22 = (bf16[12,64,768]{2,1,0:T(8,128)(2,1)}, bf16[12,64,768]{2,1,0:T(8,128)(2,1)}, u32[]{:S(2)}, u32[]{:S(2)}) collective-permute-start(bf16[12,64,768]{2,1,0:T(8,128)(2,1)} %get-tuple-element.71), channel_id=1, source_target_pairs={{0,2},{1,3},{2,0},{3,1},{4,6},{5,7},{6,4},{7,5}} | collective-permute-start | bytes 3538952 | tf_op jit(solution)/shard_map/ppermute | solution.py:470
  213.5 64.6 %copy-start.1 = (bf16[12,64,768]{2,1,0:T(8,128)(2,1)S(1)}, bf16[12,64,768]{2,1,0:T(8,128)(2,1)}, u32[]{:S(2)}) copy-start(bf16[12,64,768]{2,1,0:T(8,128)(2,1)} %param.21) | copy-start | bytes 3538948
  213.5 72.0 %collective-permute-start.23 = (bf16[12,64,768]{2,1,0:T(8,128)(2,1)}, bf16[12,64,768]{2,1,0:T(8,128)(2,1)}, u32[]{:S(2)}, u32[]{:S(2)}) collective-permute-start(bf16[12,64,768]{2,1,0:T(8,128)(2,1)} %get-tuple-element.72), channel_id=1, source_target_pairs={{0,3},{1,2},{2,1},{3,0},{4,7},{5,6},{6,5},{7,4}} | collective-permute-start | bytes 3538952 | tf_op jit(solution)/shard_map/ppermute | solution.py:470
  285.0 63.3 %collective-permute-start.8 = (bf16[24,64,768]{2,1,0:T(8,128)(2,1)}, bf16[24,64,768]{2,1,0:T(8,128)(2,1)}, u32[]{:S(2)}, u32[]{:S(2)}) collective-permute-start(bf16[24,64,768]{2,1,0:T(8,128)(2,1)} %get-tuple-element.52), channel_id=1, source_target_pairs={{0,3},{1,2},{2,1},{3,0},{4,7},{5,6},{6,5},{7,4}} | collective-permute-start | bytes 7077896 | tf_op jit(solution)/shard_map/ppermute | solution.py:470
  285.1 126.1 %collective-permute-start = (bf16[24,64,768]{2,1,0:T(8,128)(2,1)}, bf16[24,64,768]{2,1,0:T(8,128)(2,1)}, u32[]{:S(2)}, u32[]{:S(2)}) collective-permute-start(bf16[24,64,768]{2,1,0:T(8,128)(2,1)} %get-tuple-element.40), channel_id=1, source_target_pairs={{0,1},{1,0},{2,3},{3,2},{4,5},{5,4},{6,7},{7,6}} | collective-permute-start | bytes 7077896 | tf_op jit(solution)/shard_map/ppermute | solution.py:470
  285.5 125.8 %collective-permute-start.1 = (bf16[24,64,768]{2,1,0:T(8,128)(2,1)}, bf16[24,64,768]{2,1,0:T(8,128)(2,1)}, u32[]{:S(2)}, u32[]{:S(2)}) collective-permute-start(bf16[24,64,768]{2,1,0:T(8,128)(2,1)} %get-tuple-element.41), channel_id=1, source_target_pairs={{0,2},{1,3},{2,0},{3,1},{4,6},{5,7},{6,4},{7,5}} | collective-permute-start | bytes 7077896 | tf_op jit(solution)/shard_map/ppermute | solution.py:470
  347.9 2.2 copy-start.2
  347.9 91.3 %collective-permute-start.2 = (bf16[24,64,768]{2,1,0:T(8,128)(2,1)}, bf16[24,64,768]{2,1,0:T(8,128)(2,1)}, u32[]{:S(2)}, u32[]{:S(2)}) collective-permute-start(bf16[24,64,768]{2,1,0:T(8,128)(2,1)} %get-tuple-element.42), channel_id=1, source_target_pairs={{0,3},{1,2},{2,1},{3,0},{4,7},{5,6},{6,5},{7,4}} | collective-permute-start | bytes 7077896 | tf_op jit(solution)/shard_map/ppermute | solution.py:470
  347.9 153.2 %collective-permute-start.18 = (bf16[12,64,768]{2,1,0:T(8,128)(2,1)}, bf16[12,64,768]{2,1,0:T(8,128)(2,1)}, u32[]{:S(2)}, u32[]{:S(2)}) collective-permute-start(bf16[12,64,768]{2,1,0:T(8,128)(2,1)} %get-tuple-element.66), channel_id=1, source_target_pairs={{0,1},{1,0},{2,3},{3,2},{4,5},{5,4},{6,7},{7,6}} | collective-permute-start | bytes 3538952 | tf_op jit(solution)/shard_map/ppermute | solution.py:470
  348.4 153.0 %collective-permute-start.19 = (bf16[12,64,768]{2,1,0:T(8,128)(2,1)}, bf16[12,64,768]{2,1,0:T(8,128)(2,1)}, u32[]{:S(2)}, u32[]{:S(2)}) collective-permute-start(bf16[12,64,768]{2,1,0:T(8,128)(2,1)} %get-tuple-element.67), channel_id=1, source_target_pairs={{0,2},{1,3},{2,0},{3,1},{4,6},{5,7},{6,4},{7,5}} | collective-permute-start | bytes 3538952 | tf_op jit(solution)/shard_map/ppermute | solution.py:470
  350.1 61.2 %copy-start.4 = (bf16[12,64,768]{2,1,0:T(8,128)(2,1)S(1)}, bf16[12,64,768]{2,1,0:T(8,128)(2,1)}, u32[]{:S(2)}) copy-start(bf16[12,64,768]{2,1,0:T(8,128)(2,1)} %get-tuple-element.68) | copy-start | bytes 3538948
  411.2 90.5 %collective-permute-start.20 = (bf16[12,64,768]{2,1,0:T(8,128)(2,1)S(1)}, bf16[12,64,768]{2,1,0:T(8,128)(2,1)}, u32[]{:S(2)}, u32[]{:S(2)}) collective-permute-start(bf16[12,64,768]{2,1,0:T(8,128)(2,1)S(1)} %copy-done.4), channel_id=1, source_target_pairs={{0,3},{1,2},{2,1},{3,0},{4,7},{5,6},{6,5},{7,4}} | collective-permute-start | bytes 3538952 | tf_op jit(solution)/shard_map/ppermute | solution.py:470
  411.3 152.8 %collective-permute-start.10 = (bf16[24,64,768]{2,1,0:T(8,128)(2,1)}, bf16[24,64,768]{2,1,0:T(8,128)(2,1)}, u32[]{:S(2)}, u32[]{:S(2)}) collective-permute-start(bf16[24,64,768]{2,1,0:T(8,128)(2,1)} %get-tuple-element.55), channel_id=1, source_target_pairs={{0,2},{1,3},{2,0},{3,1},{4,6},{5,7},{6,4},{7,5}} | collective-permute-start | bytes 7077896 | tf_op jit(solution)/shard_map/ppermute | solution.py:470
  439.2 151.7 %collective-permute-start.11 = (bf16[24,64,768]{2,1,0:T(8,128)(2,1)}, bf16[24,64,768]{2,1,0:T(8,128)(2,1)}, u32[]{:S(2)}, u32[]{:S(2)}) collective-permute-start(bf16[24,64,768]{2,1,0:T(8,128)(2,1)} %get-tuple-element.56), channel_id=1, source_target_pairs={{0,3},{1,2},{2,1},{3,0},{4,7},{5,6},{6,5},{7,4}} | collective-permute-start | bytes 7077896 | tf_op jit(solution)/shard_map/ppermute | solution.py:470
  439.8 61.3 %copy-start.3 = (bf16[24,64,768]{2,1,0:T(8,128)(2,1)S(1)}, bf16[24,64,768]{2,1,0:T(8,128)(2,1)}, u32[]{:S(2)}) copy-start(bf16[24,64,768]{2,1,0:T(8,128)(2,1)} %get-tuple-element.54) | copy-start | bytes 7077892
  501.1 89.7 %collective-permute-start.9 = (bf16[24,64,768]{2,1,0:T(8,128)(2,1)S(1)}, bf16[24,64,768]{2,1,0:T(8,128)(2,1)}, u32[]{:S(2)}, u32[]{:S(2)}) collective-permute-start(bf16[24,64,768]{2,1,0:T(8,128)(2,1)S(1)} %copy-done.3), channel_id=1, source_target_pairs={{0,1},{1,0},{2,3},{3,2},{4,5},{5,4},{6,7},{7,6}} | collective-permute-start | bytes 7077896 | tf_op jit(solution)/shard_map/ppermute | solution.py:470
  501.4 203.8 %collective-permute-start.3 = (bf16[24,64,768]{2,1,0:T(8,128)(2,1)}, bf16[24,64,768]{2,1,0:T(8,128)(2,1)}, u32[]{:S(2)}, u32[]{:S(2)}) collective-permute-start(bf16[24,64,768]{2,1,0:T(8,128)(2,1)} %get-tuple-element.44), channel_id=1, source_target_pairs={{0,1},{1,0},{2,3},{3,2},{4,5},{5,4},{6,7},{7,6}} | collective-permute-start | bytes 7077896 | tf_op jit(solution)/shard_map/ppermute | solution.py:470
  501.7 203.5 %collective-permute-start.4 = (bf16[24,64,768]{2,1,0:T(8,128)(2,1)}, bf16[24,64,768]{2,1,0:T(8,128)(2,1)}, u32[]{:S(2)}, u32[]{:S(2)}) collective-permute-start(bf16[24,64,768]{2,1,0:T(8,128)(2,1)} %get-tuple-element.45), channel_id=1, source_target_pairs={{0,2},{1,3},{2,0},{3,1},{4,6},{5,7},{6,4},{7,5}} | collective-permute-start | bytes 7077896 | tf_op jit(solution)/shard_map/ppermute | solution.py:470
  564.1 141.2 %collective-permute-start.5 = (bf16[24,64,768]{2,1,0:T(8,128)(2,1)}, bf16[24,64,768]{2,1,0:T(8,128)(2,1)}, u32[]{:S(2)}, u32[]{:S(2)}) collective-permute-start(bf16[24,64,768]{2,1,0:T(8,128)(2,1)} %get-tuple-element.46), channel_id=1, source_target_pairs={{0,3},{1,2},{2,1},{3,0},{4,7},{5,6},{6,5},{7,4}} | collective-permute-start | bytes 7077896 | tf_op jit(solution)/shard_map/ppermute | solution.py:470
